TPU v7x, 32 devices: a whole 2x2x4 slice. The times are simulated.
32 devices in a mesh: dp: 4 (over x, core), row: 2 (over y), col: 4 (over z).
Axes of the slice: x: 2, y: 2, z: 4, core: 2. Of those that a mesh axis runs over, the one named last changes fastest.
Arguments:
- act_in: bfloat16 [4096, 2304], P(('dp', 'row'), 'col'), may hold values from -6 to 6
- cot_out: bfloat16 [4096, 2304], P(('dp', 'row'), 'col'), may hold values from -6 to 6
- w_gate: bfloat16 [2304, 4608], P(('dp', 'row'), 'col'), may hold values from -0.125 to 0.125
- w_up: bfloat16 [2304, 4608], P(('dp', 'row'), 'col'), may hold values from -0.125 to 0.125
- w_down: bfloat16 [4608, 2304], P('col', ('dp', 'row')), may hold values from -0.09375 to 0.09375
Outputs:
- input_grad: bfloat16 [4096, 2304], P(('dp', 'row'), 'col')
- gate_grad: float32 [2304, 4608], P(('dp', 'row'), 'col')
- up_grad: float32 [2304, 4608], P(('dp', 'row'), 'col')
- down_grad: float32 [4608, 2304], P('col', ('dp', 'row'))
All inputs are finite; a program needn't handle non-finite values.
Results may differ from a plain program's by a relative error of at most 0.015.
Values may be sent and summed in bfloat16 or wider, within the bound.
A program may use at most 128 MiB of HBM per device.

v0:
```python
import math

import jax
import jax.numpy as jnp
from jax import lax
from jax.sharding import PartitionSpec as P

gelu_cubic = 0.044715
gelu_scale = 0.7978845608028654


def gelu_parts(values):
    inner_arg = gelu_scale * (values + gelu_cubic * values * values * values)
    tanh_val = jnp.tanh(inner_arg)
    output = 0.5 * values * (1.0 + tanh_val)
    slope_val = 0.5 * (1.0 + tanh_val) + 0.5 * values * (1.0 - tanh_val * tanh_val) * gelu_scale * (
        1.0 + 3.0 * gelu_cubic * values * values
    )
    return (output, slope_val)


def token_contract(left, right):
    return lax.dot_general(
        left, right, (((0,), (0,)), ((), ())), preferred_element_type=jnp.float32
    )


def body(act_in, cot_out, w_gate, w_up, w_down):
    tok_rows = act_in.shape[0]
    hid_cols = w_gate.shape[1]
    act_full, cot_full = (
        lax.all_gather(act_in, "col", axis=1, tiled=True),
        lax.all_gather(cot_out, "col", axis=1, tiled=True),
    )
    gate_cols, up_cols = (
        lax.all_gather(w_gate, ("dp", "row"), axis=0, tiled=True),
        lax.all_gather(w_up, ("dp", "row"), axis=0, tiled=True),
    )
    gate_pre = jnp.dot(act_full, gate_cols, preferred_element_type=jnp.float32)
    up_pre = jnp.dot(act_full, up_cols, preferred_element_type=jnp.float32)
    cot_block = cot_full
    hidden_grad = lax.dot_general(
        cot_block,
        lax.all_gather(w_down, ("dp", "row"), axis=1, tiled=True),
        (((1,), (1,)), ((), ())),
        preferred_element_type=jnp.float32,
    )
    act_val, slope_val = gelu_parts(gate_pre)
    hidden = (act_val * up_pre).astype(jnp.bfloat16)
    d_gate = (hidden_grad * up_pre * slope_val).astype(jnp.bfloat16)
    d_up = (hidden_grad * act_val).astype(jnp.bfloat16)
    feature_dims = (((1,), (1,)), ((), ()))
    part_sum = lax.dot_general(d_gate, gate_cols, feature_dims, preferred_element_type=jnp.float32)
    part_sum = part_sum + lax.dot_general(
        d_up, up_cols, feature_dims, preferred_element_type=jnp.float32
    )
    rounded = lax.optimization_barrier(part_sum.astype(jnp.bfloat16)).astype(jnp.float32)
    input_grad = lax.psum_scatter(
        rounded.astype(jnp.bfloat16), "col", scatter_dimension=1, tiled=True
    )
    norm_scale = 1.0 / math.sqrt(tok_rows * lax.axis_size(("dp", "row")))
    cot_block = cot_full
    shares = lax.psum_scatter(
        jnp.concatenate(
            [
                token_contract(act_full, d_gate),
                token_contract(act_full, d_up),
                token_contract(cot_block, hidden),
            ],
            axis=1,
        ).astype(jnp.bfloat16),
        ("dp", "row"),
        scatter_dimension=0,
        tiled=True,
    ).astype(jnp.float32)
    gate_grad = shares[:, :hid_cols] * norm_scale
    up_grad = shares[:, hid_cols : 2 * hid_cols] * norm_scale
    down_grad = shares[:, 2 * hid_cols :].T * norm_scale
    return (input_grad, gate_grad, up_grad, down_grad)


def solution(mesh):
    placed = (
        P(("dp", "row"), "col"),
        P(("dp", "row"), "col"),
        P(("dp", "row"), "col"),
        P(("dp", "row"), "col"),
        P("col", ("dp", "row")),
    )
    return jax.shard_map(
        body,
        mesh=mesh,
        in_specs=placed,
        out_specs=(
            P(("dp", "row"), "col"),
            P(("dp", "row"), "col"),
            P(("dp", "row"), "col"),
            P("col", ("dp", "row")),
        ),
        check_vma=False,
    )
```

profile of v0, /device:TPU:0, one launch (start us, length us, event | category | flops | bytes accessed | tf_op | source)
XLA Modules:
  0.0 470.1 jit_solution(8092065288769232010)
XLA Ops:
  10.6 51.7 %all-gather.10.cloned.1.call-done = bf16[512,2304]{0,1:T(8,128)(2,1)} async-done(((bf16[512,576]{0,1:T(8,128)(2,1)}), bf16[512,2304]{0,1:T(8,128)(2,1)}) %all-gather.10.cloned.1.call-update) | async-done | bytes 2359312 | tf_op jit(solution)/shard_map/all_gather | solution.py:32
  62.3 41.9 %all-gather.12.cloned.1.call-done = bf16[2304,1152]{1,0:T(8,128)(2,1)} async-done(((bf16[288,1152]{1,0:T(8,128)(2,1)}), bf16[2304,1152]{1,0:T(8,128)(2,1)}) %all-gather.12.cloned.1.call-update) | async-done | bytes 5308432 | tf_op jit(solution)/shard_map/all_gather | solution.py:37
  104.2 7.9 %fusion.16 = f32[512,1152]{1,0:T(8,128)} fusion(bf16[512,2304]{0,1:T(8,128)(2,1)} %all-gather.10.cloned.1.call-done, bf16[2304,1152]{1,0:T(8,128)(2,1)} %all-gather.12.cloned.1.call-done), kind=kOutput, calls=%fused_computation.29 | convolution fusion | flops 2717908992 | bytes 10027008 | tf_op jit(solution)/shard_map/dot_general | solution.py:40
  112.1 35.3 %all-gather.14.cloned.1.call-done = bf16[2304,1152]{1,0:T(8,128)(2,1)} async-done(((bf16[288,1152]{1,0:T(8,128)(2,1)}), bf16[2304,1152]{1,0:T(8,128)(2,1)}) %all-gather.14.cloned.1.call-update) | async-done | bytes 5308432 | tf_op jit(solution)/shard_map/all_gather | solution.py:36
  147.4 7.2 %fusion.17 = f32[512,1152]{1,0:T(8,128)} fusion(bf16[512,2304]{0,1:T(8,128)(2,1)S(1)} %copy-done, bf16[2304,1152]{1,0:T(8,128)(2,1)} %all-gather.14.cloned.1.call-done), kind=kOutput, calls=%fused_computation.30 | convolution fusion | flops 2717908992 | bytes 10027008 | tf_op jit(solution)/shard_map/dot_general | solution.py:39
  154.6 44.2 %all-gather.6.cloned.1.call-done = bf16[512,2304]{0,1:T(8,128)(2,1)} async-done(((bf16[512,576]{0,1:T(8,128)(2,1)}), bf16[512,2304]{0,1:T(8,128)(2,1)}) %all-gather.6.cloned.1.call-update) | async-done | bytes 2359312 | tf_op jit(solution)/shard_map/all_gather | solution.py:33
  198.8 9.2 %fusion.2 = bf16[2304,1152]{0,1:T(8,128)(2,1)} fusion(bf16[512,2304]{0,1:T(8,128)(2,1)} %all-gather.6.cloned.1.call-done, f32[512,1152]{1,0:T(8,128)} %fusion.16, f32[512,1152]{1,0:T(8,128)} %fusion.17), kind=kOutput, calls=%fused_computation.6 | convolution fusion | flops 2726461440 | bytes 12386304 | tf_op jit(solution)/shard_map/dot_general | solution.py:23
  208.0 32.6 %all-gather.8.cloned.1.call-done = bf16[1152,2304]{0,1:T(8,128)(2,1)} async-done(((bf16[1152,288]{0,1:T(8,128)(2,1)}), bf16[1152,2304]{0,1:T(8,128)(2,1)}) %all-gather.8.cloned.1.call-update) | async-done | bytes 5308432 | tf_op jit(solution)/shard_map/all_gather | solution.py:44
  240.6 9.5 %multiply_convert_fusion.1 = (bf16[512,1152]{1,0:T(8,128)(2,1)S(1)}, bf16[512,1152]{1,0:T(8,128)(2,1)S(1)}) fusion(f32[512,1152]{1,0:T(8,128)} %fusion.17, f32[512,1152]{1,0:T(8,128)} %fusion.16, bf16[512,2304]{0,1:T(8,128)(2,1)} %all-gather.6.cloned.1.call-done, bf16[1152,2304]{0,1:T(8,128)(2,1)} %all-gather.8.cloned.1.call-done), kind=kOutput, calls=%fused_computation.19 | convolution fusion | flops 2731474944 | bytes 14745600 | tf_op jit(solution)/shard_map/dot_general | solution.py:42
  250.1 3.5 fusion.1
  253.6 3.5 fusion
  257.2 23.7 %pad_maximum_fusion = bf16[2304,3456]{0,1:T(8,128)(2,1)} fusion(bf16[2304,1152]{0,1:T(8,128)(2,1)S(1)} %bitcast.28, bf16[2304,1152]{0,1:T(8,128)(2,1)S(1)} %fusion.1, bf16[2304,1152]{0,1:T(8,128)(2,1)S(1)} %fusion), kind=kLoop, calls=%fused_computation | loop fusion | flops 47775744 | bytes 31850496 | tf_op jit(solution)/shard_map/concatenate | solution.py:64
  280.9 20.3 %copy.19 = bf16[2304,3456]{1,0:T(8,128)(2,1)} copy(bf16[2304,3456]{0,1:T(8,128)(2,1)} %pad_maximum_fusion) | data formatting | bytes 31850496
  301.5 1.0 copy-done.2
  302.5 5.7 %fusion.18 = f32[512,2304]{1,0:T(8,128)S(1)} fusion(bf16[512,1152]{1,0:T(8,128)(2,1)S(1)} %copy-done.2, bf16[2304,1152]{1,0:T(8,128)(2,1)} %all-gather.14.cloned.1.call-done), kind=kOutput, calls=%fused_computation.31 | convolution fusion | flops 2717908992 | bytes 11206656 | tf_op jit(solution)/shard_map/dot_general | solution.py:53
  308.3 7.1 %fusion.3 = bf16[512,2304]{1,0:T(8,128)(2,1)S(1)} fusion(f32[512,2304]{1,0:T(8,128)S(1)} %fusion.18, bf16[512,1152]{1,0:T(8,128)(2,1)S(1)} %get-tuple-element.15, bf16[2304,1152]{1,0:T(8,128)(2,1)} %all-gather.12.cloned.1.call-done), kind=kOutput, calls=%fused_computation.8 | convolution fusion | flops 2720268288 | bytes 13565952 | tf_op jit(solution)/shard_map/dot_general | solution.py:54
  315.4 2.5 copy.17
  317.9 94.8 %reduce-scatter.9.cloned.1.call-done = bf16[288,3456]{1,0:T(8,128)(2,1)} async-done(((bf16[2304,3456]{1,0:T(8,128)(2,1)}), bf16[288,3456]{1,0:T(8,128)(2,1)}) %reduce-scatter.9.cloned.1.call-update) | async-done | bytes 1990672
  412.7 3.0 copy.20
  416.0 1.6 fusion.11
  417.6 3.0 copy.16
  420.6 1.6 copy.15
  422.2 1.6 copy.14
  423.8 39.5 %reduce-scatter.7.cloned.1.call-done = bf16[576,512]{1,0:T(8,128)(2,1)} async-done(((bf16[2304,512]{1,0:T(8,128)(2,1)}), bf16[576,512]{1,0:T(8,128)(2,1)}) %reduce-scatter.7.cloned.1.call-update) | async-done | bytes 589840
  (25 shorter events, 4.0 us)
Async XLA Ops:
  7.2 55.1 %all-gather.10.cloned.1.call-start = ((), (), s32[]{:S(2)}) async-start(), calls=%async_computation.4 | async-start | bytes 2949120 | tf_op jit(solution)/shard_map/all_gather | solution.py:32
  7.9 96.3 %all-gather.12.cloned.1.call-start = ((), (), s32[]{:S(2)}) async-start(), calls=%async_computation.5 | async-start | bytes 5971968 | tf_op jit(solution)/shard_map/all_gather | solution.py:37
  8.6 138.7 %all-gather.14.cloned.1.call-start = ((), (), s32[]{:S(2)}) async-start(), calls=%async_computation.6 | async-start | bytes 5971968 | tf_op jit(solution)/shard_map/all_gather | solution.py:36
  9.4 189.4 %all-gather.6.cloned.1.call-start = ((), (), s32[]{:S(2)}) async-start(), calls=%async_computation.2 | async-start | bytes 2949120 | tf_op jit(solution)/shard_map/all_gather | solution.py:33
  10.0 230.6 %all-gather.8.cloned.1.call-start = ((), (), s32[]{:S(2)}) async-start(), calls=%async_computation.3 | async-start | bytes 5971968 | tf_op jit(solution)/shard_map/all_gather | solution.py:44
  10.5 402.1 %reduce-scatter.9.cloned.1.call-start = ((), (), s32[]{:S(2)}) async-start(), calls=%async_computation.8 | async-start | bytes 17915904
  62.3 85.1 %copy-start = (bf16[512,2304]{0,1:T(8,128)(2,1)S(1)}, bf16[512,2304]{0,1:T(8,128)(2,1)}, u32[]{:S(2)}) copy-start(bf16[512,2304]{0,1:T(8,128)(2,1)} %all-gather.10.cloned.1.call-done) | copy-start | bytes 7077892
  250.1 3.6 copy-start.1
  250.1 7.1 %slice-start = ((s8[5308416]{0:T(1024)(128)(4,1)}), s8[4194304]{0:T(1024)(128)(4,1)S(1)}, s32[]{:S(2)}) async-start(s8[5308416]{0:T(1024)(128)(4,1)} %bitcast.27), calls=%async_computation.9 | async-start | bytes 8388608
  253.6 3.6 slice-start.1
  301.2 1.3 copy-start.2
  301.3 162.0 %reduce-scatter.7.cloned.1.call-start = ((), (), s32[]{:S(2)}) async-start(), calls=%async_computation.7 | async-start | bytes 2949120
Sparse Core Ops, SparseCore 0:
  9.5 52.6 all-gather.9
  64.2 40.0 all-gather.11
  106.1 41.2 all-gather.13
  148.8 49.9 all-gather.5
  200.5 40.0 all-gather.7
  301.4 111.2 reduce-scatter.8
  415.5 47.6 reduce-scatter.6
where the time goes:
time: 471 us; the launch traced here: 470 us
  waiting for transfers between devices  343 us (73%)
  matrix products  53.6 us (11%)
  local copies, waits for them, and re-layouts  33 us (7%)
  other arithmetic  25.6 us (5%)
  between operations  14.2 us (3%)
    unnamed x9, waiting for transfers between devices  137 us
    all_gather x1, waiting for transfers between devices, body(): lax.all_gather(act_in, 'col', axis=1, tiled=True)  51.7 us
    all_gather x1, waiting for transfers between devices, body(): lax.all_gather(cot_out, 'col', axis=1, tiled=True)  44.2 us
    all_gather x1, waiting for transfers between devices, body(): lax.all_gather(w_up, ('dp', 'row'), axis=0, tiled=True)  41.9 us
    all_gather x1, waiting for transfers between devices, body(): lax.all_gather(w_gate, ('dp', 'row'), axis=0, tiled=True)  35.3 us
    unnamed x16, local copies, waits for them, and re-layouts  33 us
    all_gather x1, waiting for transfers between devices, body(): lax.all_gather(w_down, ('dp', 'row'), axis=1, tiled=True)  32.6 us
    concatenate x1, other arithmetic, body(): jnp.concatenate([token_contract(act_full, d_gate), token_contract(act_ful...  23.7 us
  transfers between devices with their start and end apart: 7, of which 7 were waited for; matrix products, arithmetic and copies ran while one was open for 11% of the time, Pallas kernels for 0%

commit v1 on v0

v1 whole, which is shorter than its diff:
```python
import functools
import math

import jax
import jax.numpy as jnp
from jax import lax
from jax.experimental import pallas as pl
from jax.experimental.pallas import tpu as pltpu
from jax.sharding import PartitionSpec as P

gelu_cubic = 0.044715
gelu_scale = 0.7978845608028654
MESH = pl.DeviceIdType.MESH
F32 = jnp.float32
BF16 = jnp.bfloat16


def gelu_parts(values):
    inner_arg = gelu_scale * (values + gelu_cubic * values * values * values)
    tanh_val = jnp.tanh(inner_arg)
    output = 0.5 * values * (1.0 + tanh_val)
    slope_val = 0.5 * (1.0 + tanh_val) + 0.5 * values * (1.0 - tanh_val * tanh_val) * gelu_scale * (
        1.0 + 3.0 * gelu_cubic * values * values
    )
    return (output, slope_val)


def tile_of(size, best):
    return best if size % best == 0 else size


def pieces_of(rows):
    if rows % 32 == 0:
        return [(0, 0, rows, 0), (1, 0, rows, 1), (2, 0, rows // 2, 0), (2, rows // 2, rows // 2, 1)]
    return [(0, 0, rows, 0), (1, 0, rows, 1), (2, 0, rows, 0)]


def others_first(n):
    return list(range(1, n)) + [0]


class Sends:
    def __init__(self, sems):
        self.sems, self.used, self.pending = sems, 0, []

    def start(self, src, dst, recv_sem, where, cond=None):
        copy = pltpu.make_async_remote_copy(
            src_ref=src,
            dst_ref=dst,
            send_sem=self.sems.at[self.used],
            recv_sem=recv_sem,
            device_id=where,
            device_id_type=MESH,
        )
        self.used += 1
        self.pending.append((cond, copy))
        guarded(cond, copy.start)

    def finish(self):
        for cond, copy in self.pending:
            guarded(cond, copy.wait_send)


def guarded(cond, action):
    if cond is None:
        action()
    else:
        pl.when(cond)(action)


def arrived(ref, sem):
    pltpu.make_async_copy(ref, ref, sem).wait()


def kernel(sizes, act_ref, cot_ref, wg_ref, wu_ref, wd_ref, ig_ref, og_ref, ou_ref, od_ref,
           full, weights, grads, stash, partner_out, sums, first_in, second_in, ig_out, ig_in,
           own_sem, send_sem, w_sem, x_sem, pair_send, pair_recv, first_sem, second_sem, ig_sem):
    n_dp, n_row, n_col, rows, hid, feats, toks = sizes
    nq, ny = n_dp // 2, n_row
    peers = nq * ny
    pieces = pieces_of(rows)
    dp, y, col = lax.axis_index("dp"), lax.axis_index("row"), lax.axis_index("col")
    q, c = dp // 2, dp % 2
    rep_of = lambda q1, c1, y1: (q1 * 2 + c1) * ny + y1
    at_q = lambda dq: lax.rem(q + dq, nq)
    at_y = lambda dy: lax.rem(y + dy, ny)
    back_q = lambda dq: lax.rem(q + nq - dq, nq)
    back_y = lambda dy: lax.rem(y + ny - dy, ny)
    me = rep_of(q, c, y)
    partner = {"dp": q * 2 + 1 - c}
    q_peer = lambda dq: {"dp": at_q(dq) * 2 + c}
    y_peer = lambda dy: {"row": at_y(dy)}

    barrier = pltpu.get_barrier_semaphore()
    friends = [partner] + [q_peer(i) for i in range(1, nq)] + [y_peer(i) for i in range(1, ny)]
    friends += [{"col": lax.rem(col + i, n_col)} for i in range(1, n_col)]
    for friend in friends:
        pl.semaphore_signal(barrier, inc=1, device_id=friend, device_id_type=MESH)
    pl.semaphore_wait(barrier, len(friends))

    sends = Sends(send_sem)
    mine = (wg_ref, wu_ref, wd_ref)
    streams = (act_ref, cot_ref)

    def rows_at(rep, r0, nr):
        return pl.ds(pl.multiple_of(rep * rows + r0, 8), nr)

    def slot(p, rep):
        w, r0, nr, _ = pieces[p]
        return weights.at[w, rows_at(rep, r0, nr), :]

    def feat_slot(s, block):
        return full.at[s, pl.ds(pl.multiple_of(block * feats, 8), feats), :]

    has_right, has_left = col < n_col - 1, col > 0
    right = {"col": jnp.minimum(col + 1, n_col - 1)}
    left = {"col": jnp.maximum(col - 1, 0)}
    for s in range(2):
        sends.start(streams[s], feat_slot(s, col), x_sem.at[s * n_col + col], right, has_right)
        sends.start(streams[s], feat_slot(s, col), x_sem.at[s * n_col + col], left, has_left)
    for p, (w, r0, nr, route) in enumerate(pieces):
        src = mine[w].at[pl.ds(r0, nr), :]
        sem = w_sem.at[p * peers * 2 + me]
        for dq in range(1, nq):
            sends.start(src, slot(p, me), sem, q_peer(dq))
        for dy in range(1, ny):
            sends.start(src, slot(p, me), sem, y_peer(dy))
        sends.start(src, slot(p, me), sem, partner)
    locals_ = []
    for i, (src, dst) in enumerate(
        [(streams[s], feat_slot(s, col)) for s in range(2)]
        + [(mine[w], weights.at[w, rows_at(me, 0, rows), :]) for w in range(3)]
    ):
        locals_.append(pltpu.make_async_copy(src, dst, own_sem.at[i]))
        locals_[-1].start()

    def chain(s, step):
        from_left, from_right = col >= step, col + step < n_col
        lb, rb = jnp.maximum(col - step, 0), jnp.minimum(col + step, n_col - 1)
        l_sem, r_sem = x_sem.at[s * n_col + lb], x_sem.at[s * n_col + rb]
        guarded(from_left, lambda: arrived(feat_slot(s, lb), l_sem))
        if step < n_col - 1:
            sends.start(feat_slot(s, lb), feat_slot(s, lb), l_sem, right, from_left & has_right)
        guarded(from_right, lambda: arrived(feat_slot(s, rb), r_sem))
        if step < n_col - 1:
            sends.start(feat_slot(s, rb), feat_slot(s, rb), r_sem, left, from_right & has_left)

    def take(p, rep, forward):
        sem = w_sem.at[p * peers * 2 + rep]
        arrived(slot(p, rep), sem)
        for where in forward + [partner]:
            sends.start(slot(p, rep), slot(p, rep), sem, where)

    def near(p):
        route = pieces[p][3]
        for dq in range(1, nq):
            take(p, rep_of(back_q(dq), c, y), [y_peer(i) for i in range(1, ny)] if route == 0 else [])
        for dy in range(1, ny):
            take(p, rep_of(q, c, back_y(dy)), [q_peer(i) for i in range(1, nq)] if route == 1 else [])

    def far(p):
        for dq in range(1, nq):
            for dy in range(1, ny):
                take(p, rep_of(back_q(dq), c, back_y(dy)), [])

    def from_partner(p):
        for dq in range(nq):
            for dy in range(ny):
                rep = rep_of(at_q(dq), 1 - c, at_y(dy))
                arrived(slot(p, rep), w_sem.at[p * peers * 2 + rep])

    todo = [functools.partial(near, p) for p in range(len(pieces))]
    todo += [functools.partial(far, p) for p in range(len(pieces))]
    chains = [functools.partial(chain, s, step) for step in range(1, n_col) for s in range(2)]
    while len(chains) > 1 or todo:
        if len(chains) > 1:
            chains.pop(0)()
        if todo:
            todo.pop(0)()
    for p in range(len(pieces)):
        from_partner(p)
    for copy in locals_:
        copy.wait()

    mt, nt = tile_of(toks, 256), tile_of(hid, 384)
    m_tiles, n_tiles = toks // mt, hid // nt
    token_dims = (((0,), (0,)), ((), ()))

    def tile_slices(i):
        m, n = i // n_tiles, i % n_tiles
        return pl.ds(pl.multiple_of(m * mt, mt), mt), pl.ds(pl.multiple_of(n * nt, nt), nt)

    @pl.loop(0, m_tiles * n_tiles)
    def _(i):
        ms, ns = tile_slices(i)
        x = full[0, :, ms]
        gate_pre = lax.dot_general(x, weights[0, :, ns], token_dims, preferred_element_type=F32)
        up_pre = lax.dot_general(x, weights[1, :, ns], token_dims, preferred_element_type=F32)
        act_val, slope_val = gelu_parts(gate_pre)
        grads[2, ms, ns] = (act_val * up_pre).astype(BF16)
        stash[0, ms, ns] = up_pre * slope_val
        stash[1, ms, ns] = act_val

    chains.pop(0)()

    @pl.loop(0, m_tiles * n_tiles)
    def _(i):
        ms, ns = tile_slices(i)
        hidden_grad = lax.dot_general(full[1, :, ms], weights[2, :, ns], token_dims, preferred_element_type=F32)
        grads[0, ms, ns] = (hidden_grad * stash[0, ms, ns]).astype(BF16)
        grads[1, ms, ns] = (hidden_grad * stash[1, ms, ns]).astype(BF16)

    def term(w, rep, ns):
        return jnp.dot(full[w // 2, rows_at(rep, 0, rows), :], grads[w, :, ns], preferred_element_type=F32)

    def n_slice(n):
        return pl.ds(pl.multiple_of(n * nt, nt), nt)

    def pair_copy(i):
        return pltpu.make_async_remote_copy(
            src_ref=partner_out.at[i],
            dst_ref=sums.at[i],
            send_sem=pair_send.at[i],
            recv_sem=pair_recv.at[i],
            device_id=partner,
            device_id_type=MESH,
        )

    @pl.loop(0, 3 * peers)
    def _(i):
        w, peer = i // peers, i % peers
        rep = rep_of(peer // ny, 1 - c, peer % ny)

        @pl.loop(0, n_tiles)
        def _(n):
            partner_out[i, :, n_slice(n)] = term(w, rep, n_slice(n)).astype(BF16)

        pair_copy(i).start()

    first_base, count = [], 0
    for _, _, _, route in pieces:
        first_base.append(count)
        count += (nq - 1) * ny if route == 0 else (ny - 1) * nq
    second_base, count = [], 0
    for _, _, _, route in pieces:
        second_base.append(count)
        count += (ny - 1) if route == 0 else (nq - 1)

    def first_slot(p, dq, dy):
        k = first_base[p] + ((dq - 1) * ny + dy if pieces[p][3] == 0 else (dy - 1) * nq + dq)
        return first_in.at[k, pl.ds(0, pieces[p][2]), :], first_sem.at[k]

    def second_slot(p, d):
        k = second_base[p] + d - 1
        return second_in.at[k, pl.ds(0, pieces[p][2]), :], second_sem.at[k]

    for w in range(3):
        for dq in others_first(nq):
            for dy in others_first(ny):
                index = w * peers + at_q(dq) * ny + at_y(dy)
                rep = rep_of(at_q(dq), c, at_y(dy))
                arrived(sums.at[index], pair_recv.at[index])

                @pl.loop(0, n_tiles)
                def _(n):
                    ns = n_slice(n)
                    sums[index, :, ns] = (term(w, rep, ns) + sums[index, :, ns].astype(F32)).astype(BF16)

                for p, (pw, r0, nr, route) in enumerate(pieces):
                    if pw == w and (dq if route == 0 else dy):
                        dst, sem = first_slot(p, dq, dy)
                        where = q_peer(dq) if route == 0 else y_peer(dy)
                        sends.start(sums.at[index, pl.ds(r0, nr), :], dst, sem, where)

    rt = tile_of(feats, 288)
    hid_dims = (((1,), (1,)), ((), ()))
    for dz in others_first(n_col):
        block = lax.rem(col + dz, n_col)

        @pl.loop(0, feats // rt)
        def _(r):
            rs = pl.ds(pl.multiple_of(block * feats + r * rt, 8), rt)
            part = lax.dot_general(weights[0, rs, :], grads[0], hid_dims, preferred_element_type=F32)
            part = part + lax.dot_general(weights[1, rs, :], grads[1], hid_dims, preferred_element_type=F32)
            ig_out[dz, pl.ds(pl.multiple_of(r * rt, 8), rt), :] = part.astype(BF16)

        if dz:
            sends.start(ig_out.at[dz], ig_in.at[dz - 1], ig_sem.at[dz - 1], {"col": block})

    outs = (og_ref, ou_ref, od_ref)
    for p, (w, r0, nr, route) in enumerate(pieces):
        rs = pl.ds(r0, nr)
        n_first, n_second = (nq, ny) if route == 0 else (ny, nq)
        for d in others_first(n_second):
            index = w * peers + (q * ny + at_y(d) if route == 0 else at_q(d) * ny + y)
            total = sums[index, rs, :].astype(F32)
            for f in range(1, n_first):
                ref, sem = first_slot(p, f, d) if route == 0 else first_slot(p, d, f)
                arrived(ref, sem)
                total = total + ref[...].astype(F32)
            if d:
                sums[index, rs, :] = total.astype(BF16)
                dst, sem = second_slot(p, d)
                sends.start(sums.at[index, rs, :], dst, sem, y_peer(d) if route == 0 else q_peer(d))
            else:
                outs[w][rs, :] = total

    total = ig_out[0].astype(F32)
    for dz in range(1, n_col):
        arrived(ig_in.at[dz - 1], ig_sem.at[dz - 1])
        total = total + ig_in[dz - 1].astype(F32)
    ig_ref[...] = total.astype(BF16)

    for p, (w, r0, nr, route) in enumerate(pieces):
        rs = pl.ds(r0, nr)
        for d in range(1, ny if route == 0 else nq):
            ref, sem = second_slot(p, d)
            arrived(ref, sem)
            outs[w][rs, :] = outs[w][rs, :] + ref[...].astype(F32)

    sends.finish()

    @pl.loop(0, 3 * peers)
    def _(i):
        pair_copy(i).wait_send()


def body(n_dp, n_row, n_col, act_in, cot_out, w_gate, w_up, w_down):
    toks, feats = act_in.shape
    rows, hid = w_gate.shape
    sizes = (n_dp, n_row, n_col, rows, hid, feats, toks)
    nq, ny = n_dp // 2, n_row
    peers, reps, dim = nq * ny, n_dp * n_row, feats * n_col
    pieces = pieces_of(rows)
    firsts = sum((nq - 1) * ny if r == 0 else (ny - 1) * nq for _, _, _, r in pieces)
    seconds = sum((ny - 1) if r == 0 else (nq - 1) for _, _, _, r in pieces)
    near_far = sum((nq - 1) * (ny - 1) for _ in pieces)
    n_sends = 4 + 4 * (n_col - 2) + len(pieces) * (nq + ny - 1) + len(pieces) * (peers - 1) + near_far
    n_sends += firsts + seconds + n_col - 1
    any_spec, vmem_spec = pl.BlockSpec(memory_space=pl.ANY), pl.BlockSpec(memory_space=pltpu.VMEM)
    dma = lambda n: pltpu.SemaphoreType.DMA((max(n, 1),))
    wgrad = jax.ShapeDtypeStruct((rows, hid), F32)
    ig_t, gate_grad, up_grad, down_t = pl.pallas_call(
        functools.partial(kernel, sizes),
        out_shape=[jax.ShapeDtypeStruct((feats, toks), BF16), wgrad, wgrad, wgrad],
        in_specs=[any_spec] * 5,
        out_specs=[vmem_spec] * 4,
        scratch_shapes=[
            pltpu.VMEM((2, dim, toks), BF16),
            pltpu.VMEM((3, dim, hid), BF16),
            pltpu.VMEM((3, toks, hid), BF16),
            pltpu.VMEM((2, toks, hid), F32),
            pltpu.VMEM((3 * peers, rows, hid), BF16),
            pltpu.VMEM((3 * peers, rows, hid), BF16),
            pltpu.VMEM((max(firsts, 1), rows, hid), BF16),
            pltpu.VMEM((max(seconds, 1), rows, hid), BF16),
            pltpu.VMEM((n_col, feats, toks), BF16),
            pltpu.VMEM((max(n_col - 1, 1), feats, toks), BF16),
            dma(5), dma(n_sends), dma(len(pieces) * reps), dma(2 * n_col), dma(3 * peers), dma(3 * peers),
            dma(firsts), dma(seconds), dma(n_col - 1),
        ],
        compiler_params=pltpu.CompilerParams(
            collective_id=0, has_side_effects=True, vmem_limit_bytes=67043328
        ),
    )(act_in.T, cot_out.T, w_gate, w_up, w_down.T)
    norm_scale = 1.0 / math.sqrt(toks * n_dp * n_row)
    return (ig_t.T, gate_grad * norm_scale, up_grad * norm_scale, (down_t * norm_scale).T)


def solution(mesh):
    grid = P(("dp", "row"), "col")
    flipped = P("col", ("dp", "row"))
    return jax.shard_map(
        functools.partial(body, mesh.shape["dp"], mesh.shape["row"], mesh.shape["col"]),
        mesh=mesh,
        in_specs=(grid, grid, grid, grid, flipped),
        out_specs=(grid, grid, grid, flipped),
        check_vma=False,
    )
```

time: 471 us -> 180 us (0.38)
  waiting for transfers between devices: 343 us -> 0 us
  Pallas kernels: 0 us -> 174 us
  matrix products: 53.6 us -> 0 us
  local copies, waits for them, and re-layouts: 33 us -> 0.83 us
  other arithmetic: 25.6 us -> 4.29 us
  between operations: 14.2 us -> 0.66 us
    all_gather x5 -> x0, waiting for transfers between devices: 206 us -> none  [the longest x1 51.7 us: body(): lax.all_gather(act_in, 'col', axis=1, tiled=True)]
    pallas_call x0 -> x1, Pallas kernels: none -> 174 us  [body(): pl.pallas_call(functools.partial(kernel, sizes), out_shape=[jax.ShapeDtyp...]
    unnamed x9 -> x0, waiting for transfers between devices: 137 us -> none
    dot_general x8 -> x0, matrix products: 53.6 us -> none  [the longest x3 16.2 us: token_contract(): lax.dot_general(left, right, (((0,), (0,)), ((), ())), preferred_element_...]
    unnamed x16 -> x7, local copies, waits for them, and re-layouts: 33 us -> 0.83 us
    concatenate x1 -> x0, other arithmetic: 23.7 us -> none  [body(): jnp.concatenate([token_contract(act_full, d_gate), token_contract(act_ful...]
  transfers between devices with their start and end apart: 7 -> 0, of which waited for: 7 -> 0; matrix products, arithmetic and copies ran while one was open for 11% -> 0% of each run, Pallas kernels for 0% -> 0%
where the time goes in v1:
time: 180 us; the launch traced here: 179 us
  Pallas kernels  174 us (97%)
  other arithmetic  4.29 us (2%)
    pallas_call x1, Pallas kernels, body(): pl.pallas_call(functools.partial(kernel, sizes), out_shape=[jax.ShapeDtyp...  174 us

profile of v1, /device:TPU:0, one launch (start us, length us, event | category | flops | bytes accessed | tf_op | source)
XLA Modules:
  0.0 179.4 jit_solution(3528745797543360484)
XLA Ops:
  0.6 173.6 %shard_map.84 = (bf16[576,512]{1,0:T(8,128)(2,1)}, f32[288,1152]{1,0:T(8,128)}, f32[288,1152]{1,0:T(8,128)}, f32[288,1152]{1,0:T(8,128)}) custom-call(bf16[576,512]{1,0:T(8,128)(2,1)} %bitcast.8, bf16[576,512]{1,0:T(8,128)(2,1)} %bitcast.9, bf16[288,1152]{1,0:T(8,128)(2,1)} %wg_ref.1, bf16[288,1152]{1,0:T(8,128)(2,1)} %wu_ref.1, bf16[288,1152]{1,0:T(8,128)(2,1)} %bitcast.6), custom_call_target="tpu_custom_call" | custom-call | tf_op jit(solution)/shard_map/pallas_call | solution.py:343
  174.3 0.0 copy-start
  174.3 0.0 copy-start.1
  174.3 2.6 %broadcast_multiply_fusion.1 = f32[288,1152]{1,0:T(8,128)} fusion(f32[288,1152]{1,0:T(8,128)} %get-tuple-element.9), kind=kLoop, calls=%fused_computation.2 | loop fusion | flops 331776 | bytes 2654208 | tf_op jit(solution)/shard_map/mul | solution.py:367
  176.9 0.0 copy-done
  176.9 0.0 copy-done.1
  176.9 0.0 copy-start.2
  176.9 1.7 multiply_bitcast_fusion
  178.6 0.0 copy-done.2
  178.6 0.8 copy.10
Async XLA Ops:
  174.3 2.6 %copy-start = (f32[288,1152]{1,0:T(8,128)S(1)}, f32[288,1152]{1,0:T(8,128)}, u32[]{:S(2)}) copy-start(f32[288,1152]{1,0:T(8,128)} %get-tuple-element.10) | copy-start | bytes 3981316
  174.3 2.6 %copy-start.1 = (f32[288,1152]{1,0:T(8,128)S(1)}, f32[288,1152]{1,0:T(8,128)}, u32[]{:S(2)}) copy-start(f32[288,1152]{1,0:T(8,128)} %get-tuple-element.11) | copy-start | bytes 3981316
  176.9 1.7 copy-start.2

commit v2 on v1

--- a/solution.py
+++ b/solution.py
@@ -109,26 +109,42 @@
         w, r0, nr, _ = pieces[p]
         return weights.at[w, rows_at(rep, r0, nr), :]
 
-    def feat_slot(s, block):
-        return full.at[s, pl.ds(pl.multiple_of(block * feats, 8), feats), :]
+    half = feats // 2
+
+    def feat_slot(s, h, block):
+        return full.at[s, pl.ds(pl.multiple_of(block * feats + h * half, 8), half), :]
+
+    def feat_sem(s, h, block):
+        return x_sem.at[(s * 2 + h) * n_col + block]
 
     has_right, has_left = col < n_col - 1, col > 0
     right = {"col": jnp.minimum(col + 1, n_col - 1)}
     left = {"col": jnp.maximum(col - 1, 0)}
-    for s in range(2):
-        sends.start(streams[s], feat_slot(s, col), x_sem.at[s * n_col + col], right, has_right)
-        sends.start(streams[s], feat_slot(s, col), x_sem.at[s * n_col + col], left, has_left)
-    for p, (w, r0, nr, route) in enumerate(pieces):
-        src = mine[w].at[pl.ds(r0, nr), :]
-        sem = w_sem.at[p * peers * 2 + me]
-        for dq in range(1, nq):
-            sends.start(src, slot(p, me), sem, q_peer(dq))
-        for dy in range(1, ny):
-            sends.start(src, slot(p, me), sem, y_peer(dy))
-        sends.start(src, slot(p, me), sem, partner)
+
+    def own_features(s):
+        for h in range(2):
+            src = streams[s].at[pl.ds(h * half, half), :]
+            sends.start(src, feat_slot(s, h, col), feat_sem(s, h, col), right, has_right)
+            sends.start(src, feat_slot(s, h, col), feat_sem(s, h, col), left, has_left)
+
+    def own_weight(weight):
+        for p, (w, r0, nr, route) in enumerate(pieces):
+            if w != weight:
+                continue
+            src = mine[w].at[pl.ds(r0, nr), :]
+            sem = w_sem.at[p * peers * 2 + me]
+            for dq in range(1, nq):
+                sends.start(src, slot(p, me), sem, q_peer(dq))
+            for dy in range(1, ny):
+                sends.start(src, slot(p, me), sem, y_peer(dy))
+            sends.start(src, slot(p, me), sem, partner)
+
+    own_features(0)
+    own_weight(0)
+    own_weight(1)
     locals_ = []
     for i, (src, dst) in enumerate(
-        [(streams[s], feat_slot(s, col)) for s in range(2)]
+        [(streams[s], full.at[s, pl.ds(pl.multiple_of(col * feats, 8), feats), :]) for s in range(2)]
         + [(mine[w], weights.at[w, rows_at(me, 0, rows), :]) for w in range(3)]
     ):
         locals_.append(pltpu.make_async_copy(src, dst, own_sem.at[i]))
@@ -137,13 +153,15 @@
     def chain(s, step):
         from_left, from_right = col >= step, col + step < n_col
         lb, rb = jnp.maximum(col - step, 0), jnp.minimum(col + step, n_col - 1)
-        l_sem, r_sem = x_sem.at[s * n_col + lb], x_sem.at[s * n_col + rb]
-        guarded(from_left, lambda: arrived(feat_slot(s, lb), l_sem))
-        if step < n_col - 1:
-            sends.start(feat_slot(s, lb), feat_slot(s, lb), l_sem, right, from_left & has_right)
-        guarded(from_right, lambda: arrived(feat_slot(s, rb), r_sem))
-        if step < n_col - 1:
-            sends.start(feat_slot(s, rb), feat_slot(s, rb), r_sem, left, from_right & has_left)
+        for h in range(2):
+            l_slot, l_sem = feat_slot(s, h, lb), feat_sem(s, h, lb)
+            r_slot, r_sem = feat_slot(s, h, rb), feat_sem(s, h, rb)
+            guarded(from_left, lambda: arrived(l_slot, l_sem))
+            if step < n_col - 1:
+                sends.start(l_slot, l_slot, l_sem, right, from_left & has_right)
+            guarded(from_right, lambda: arrived(r_slot, r_sem))
+            if step < n_col - 1:
+                sends.start(r_slot, r_slot, r_sem, left, from_right & has_left)
 
     def take(p, rep, forward):
         sem = w_sem.at[p * peers * 2 + rep]
@@ -169,46 +187,50 @@
                 rep = rep_of(at_q(dq), 1 - c, at_y(dy))
                 arrived(slot(p, rep), w_sem.at[p * peers * 2 + rep])
 
-    todo = [functools.partial(near, p) for p in range(len(pieces))]
-    todo += [functools.partial(far, p) for p in range(len(pieces))]
-    chains = [functools.partial(chain, s, step) for step in range(1, n_col) for s in range(2)]
-    while len(chains) > 1 or todo:
-        if len(chains) > 1:
-            chains.pop(0)()
-        if todo:
-            todo.pop(0)()
-    for p in range(len(pieces)):
-        from_partner(p)
+    near(0)
+    chain(0, 1)
+    near(1)
+    own_weight(2)
+    for step in range(2, n_col):
+        if step == n_col - 1:
+            own_features(1)
+        chain(0, step)
+    far(0)
+    far(1)
+    from_partner(0)
+    from_partner(1)
     for copy in locals_:
         copy.wait()
 
     mt, nt = tile_of(toks, 256), tile_of(hid, 384)
     m_tiles, n_tiles = toks // mt, hid // nt
     token_dims = (((0,), (0,)), ((), ()))
+    later = [p for p in range(len(pieces)) if pieces[p][0] == 2]
 
     def tile_slices(i):
         m, n = i // n_tiles, i % n_tiles
         return pl.ds(pl.multiple_of(m * mt, mt), mt), pl.ds(pl.multiple_of(n * nt, nt), nt)
 
-    @pl.loop(0, m_tiles * n_tiles)
-    def _(i):
-        ms, ns = tile_slices(i)
-        x = full[0, :, ms]
-        gate_pre = lax.dot_general(x, weights[0, :, ns], token_dims, preferred_element_type=F32)
-        up_pre = lax.dot_general(x, weights[1, :, ns], token_dims, preferred_element_type=F32)
-        act_val, slope_val = gelu_parts(gate_pre)
-        grads[2, ms, ns] = (act_val * up_pre).astype(BF16)
-        stash[0, ms, ns] = up_pre * slope_val
-        stash[1, ms, ns] = act_val
-
-    chains.pop(0)()
-
-    @pl.loop(0, m_tiles * n_tiles)
-    def _(i):
-        ms, ns = tile_slices(i)
-        hidden_grad = lax.dot_general(full[1, :, ms], weights[2, :, ns], token_dims, preferred_element_type=F32)
-        grads[0, ms, ns] = (hidden_grad * stash[0, ms, ns]).astype(BF16)
-        grads[1, ms, ns] = (hidden_grad * stash[1, ms, ns]).astype(BF16)
+    def project(first, last):
+        @pl.loop(first, last)
+        def _(i):
+            ms, ns = tile_slices(i)
+            x = full[0, :, ms]
+            gate_pre = lax.dot_general(x, weights[0, :, ns], token_dims, preferred_element_type=F32)
+            up_pre = lax.dot_general(x, weights[1, :, ns], token_dims, preferred_element_type=F32)
+            act_val, slope_val = gelu_parts(gate_pre)
+            grads[2, ms, ns] = (act_val * up_pre).astype(BF16)
+            stash[0, ms, ns] = up_pre * slope_val
+            stash[1, ms, ns] = act_val
+
+    tiles = m_tiles * n_tiles
+    project(0, tiles // 2)
+    chain(1, 1)
+    project(tiles // 2, tiles)
+    for p in later:
+        near(p)
+    for step in range(2, n_col - 1):
+        chain(1, step)
 
     def term(w, rep, ns):
         return jnp.dot(full[w // 2, rows_at(rep, 0, rows), :], grads[w, :, ns], preferred_element_type=F32)
@@ -226,16 +248,24 @@
             device_id_type=MESH,
         )
 
-    @pl.loop(0, 3 * peers)
-    def _(i):
-        w, peer = i // peers, i % peers
-        rep = rep_of(peer // ny, 1 - c, peer % ny)
-
-        @pl.loop(0, n_tiles)
-        def _(n):
-            partner_out[i, :, n_slice(n)] = term(w, rep, n_slice(n)).astype(BF16)
-
-        pair_copy(i).start()
+    def is_far(rep):
+        block = (rep * rows) // feats
+        return jnp.abs(block - col) == n_col - 1
+
+    def partner_terms(w, when=None):
+        @pl.loop(0, peers)
+        def _(peer):
+            i = w * peers + peer
+            rep = rep_of(peer // ny, 1 - c, peer % ny)
+
+            def one():
+                @pl.loop(0, n_tiles)
+                def _(n):
+                    partner_out[i, :, n_slice(n)] = term(w, rep, n_slice(n)).astype(BF16)
+
+                pair_copy(i).start()
+
+            guarded(None if when is None else when(rep), one)
 
     first_base, count = [], 0
     for _, _, _, route in pieces:
@@ -254,27 +284,32 @@
         k = second_base[p] + d - 1
         return second_in.at[k, pl.ds(0, pieces[p][2]), :], second_sem.at[k]
 
-    for w in range(3):
+    def own_terms(w, when=None):
         for dq in others_first(nq):
             for dy in others_first(ny):
                 index = w * peers + at_q(dq) * ny + at_y(dy)
                 rep = rep_of(at_q(dq), c, at_y(dy))
-                arrived(sums.at[index], pair_recv.at[index])
-
-                @pl.loop(0, n_tiles)
-                def _(n):
-                    ns = n_slice(n)
-                    sums[index, :, ns] = (term(w, rep, ns) + sums[index, :, ns].astype(F32)).astype(BF16)
-
+                cond = None if when is None else when(rep)
+
+                def one():
+                    arrived(sums.at[index], pair_recv.at[index])
+
+                    @pl.loop(0, n_tiles)
+                    def _(n):
+                        ns = n_slice(n)
+                        sums[index, :, ns] = (term(w, rep, ns) + sums[index, :, ns].astype(F32)).astype(BF16)
+
+                guarded(cond, one)
                 for p, (pw, r0, nr, route) in enumerate(pieces):
                     if pw == w and (dq if route == 0 else dy):
                         dst, sem = first_slot(p, dq, dy)
                         where = q_peer(dq) if route == 0 else y_peer(dy)
-                        sends.start(sums.at[index, pl.ds(r0, nr), :], dst, sem, where)
+                        sends.start(sums.at[index, pl.ds(r0, nr), :], dst, sem, where, cond)
 
     rt = tile_of(feats, 288)
     hid_dims = (((1,), (1,)), ((), ()))
-    for dz in others_first(n_col):
+
+    def input_part(dz):
         block = lax.rem(col + dz, n_col)
 
         @pl.loop(0, feats // rt)
@@ -288,7 +323,9 @@
             sends.start(ig_out.at[dz], ig_in.at[dz - 1], ig_sem.at[dz - 1], {"col": block})
 
     outs = (og_ref, ou_ref, od_ref)
-    for p, (w, r0, nr, route) in enumerate(pieces):
+
+    def second(p):
+        w, r0, nr, route = pieces[p]
         rs = pl.ds(r0, nr)
         n_first, n_second = (nq, ny) if route == 0 else (ny, nq)
         for d in others_first(n_second):
@@ -305,6 +342,41 @@
             else:
                 outs[w][rs, :] = total
 
+    near_rep = lambda rep: jnp.logical_not(is_far(rep))
+    partner_terms(2, near_rep)
+    own_terms(2, near_rep)
+    for p in later:
+        far(p)
+    for p in later:
+        from_partner(p)
+    chain(1, n_col - 1)
+    partner_terms(2, is_far)
+
+    @pl.loop(0, tiles)
+    def _(i):
+        ms, ns = tile_slices(i)
+        hidden_grad = lax.dot_general(full[1, :, ms], weights[2, :, ns], token_dims, preferred_element_type=F32)
+        grads[0, ms, ns] = (hidden_grad * stash[0, ms, ns]).astype(BF16)
+        grads[1, ms, ns] = (hidden_grad * stash[1, ms, ns]).astype(BF16)
+
+    own_terms(2, is_far)
+    spare = list(range(1, n_col))
+    partner_terms(0)
+    input_part(spare.pop(0))
+    own_terms(0)
+    if spare:
+        input_part(spare.pop(0))
+    partner_terms(1)
+    for p in later:
+        second(p)
+    while spare:
+        input_part(spare.pop(0))
+    own_terms(1)
+    input_part(0)
+    for p in range(len(pieces)):
+        if p not in later:
+            second(p)
+
     total = ig_out[0].astype(F32)
     for dz in range(1, n_col):
         arrived(ig_in.at[dz - 1], ig_sem.at[dz - 1])
@@ -335,8 +407,8 @@
     firsts = sum((nq - 1) * ny if r == 0 else (ny - 1) * nq for _, _, _, r in pieces)
     seconds = sum((ny - 1) if r == 0 else (nq - 1) for _, _, _, r in pieces)
     near_far = sum((nq - 1) * (ny - 1) for _ in pieces)
-    n_sends = 4 + 4 * (n_col - 2) + len(pieces) * (nq + ny - 1) + len(pieces) * (peers - 1) + near_far
-    n_sends += firsts + seconds + n_col - 1
+    n_sends = 8 + 8 * (n_col - 2) + len(pieces) * (nq + ny - 1) + len(pieces) * (peers - 1) + near_far
+    n_sends += 2 * firsts + seconds + n_col - 1
     any_spec, vmem_spec = pl.BlockSpec(memory_space=pl.ANY), pl.BlockSpec(memory_space=pltpu.VMEM)
     dma = lambda n: pltpu.SemaphoreType.DMA((max(n, 1),))
     wgrad = jax.ShapeDtypeStruct((rows, hid), F32)
@@ -356,7 +428,7 @@
             pltpu.VMEM((max(seconds, 1), rows, hid), BF16),
             pltpu.VMEM((n_col, feats, toks), BF16),
             pltpu.VMEM((max(n_col - 1, 1), feats, toks), BF16),
-            dma(5), dma(n_sends), dma(len(pieces) * reps), dma(2 * n_col), dma(3 * peers), dma(3 * peers),
+            dma(5), dma(n_sends), dma(len(pieces) * reps), dma(4 * n_col), dma(3 * peers), dma(3 * peers),
             dma(firsts), dma(seconds), dma(n_col - 1),
         ],
         compiler_params=pltpu.CompilerParams(

time: 180 us -> 171 us (0.950)
  Pallas kernels: 174 us -> 166 us
    pallas_call x1, Pallas kernels: 174 us -> 166 us  [body(): pl.pallas_call(functools.partial(kernel, sizes), out_shape=[jax.ShapeDtyp...]
where the time goes in v2:
time: 171 us
  Pallas kernels  166 us (97%)
  other arithmetic  4.29 us (3%)
    pallas_call x1, Pallas kernels, body(): pl.pallas_call(functools.partial(kernel, sizes), out_shape=[jax.ShapeDtyp...  166 us

profile of v2, /device:TPU:0, one launch (start us, length us, event | category | flops | bytes accessed | tf_op | source)
XLA Modules:
  0.0 171.3 jit_solution(1872229385237373867)
XLA Ops:
  0.6 165.5 %shard_map.84 = (bf16[576,512]{1,0:T(8,128)(2,1)}, f32[288,1152]{1,0:T(8,128)}, f32[288,1152]{1,0:T(8,128)}, f32[288,1152]{1,0:T(8,128)}) custom-call(bf16[576,512]{1,0:T(8,128)(2,1)} %bitcast.8, bf16[576,512]{1,0:T(8,128)(2,1)} %bitcast.9, bf16[288,1152]{1,0:T(8,128)(2,1)} %wg_ref.1, bf16[288,1152]{1,0:T(8,128)(2,1)} %wu_ref.1, bf16[288,1152]{1,0:T(8,128)(2,1)} %bitcast.6), custom_call_target="tpu_custom_call" | custom-call | tf_op jit(solution)/shard_map/pallas_call | solution.py:415
  166.2 0.0 copy-start
  166.2 0.0 copy-start.1
  166.2 2.6 %broadcast_multiply_fusion.1 = f32[288,1152]{1,0:T(8,128)} fusion(f32[288,1152]{1,0:T(8,128)} %get-tuple-element.9), kind=kLoop, calls=%fused_computation.2 | loop fusion | flops 331776 | bytes 2654208 | tf_op jit(solution)/shard_map/mul | solution.py:439
  168.8 0.0 copy-done
  168.8 0.0 copy-done.1
  168.8 0.0 copy-start.2
  168.8 1.7 multiply_bitcast_fusion
  170.5 0.0 copy-done.2
  170.5 0.8 copy.10
Async XLA Ops:
  166.2 2.6 %copy-start = (f32[288,1152]{1,0:T(8,128)S(1)}, f32[288,1152]{1,0:T(8,128)}, u32[]{:S(2)}) copy-start(f32[288,1152]{1,0:T(8,128)} %get-tuple-element.10) | copy-start | bytes 3981316
  166.2 2.6 %copy-start.1 = (f32[288,1152]{1,0:T(8,128)S(1)}, f32[288,1152]{1,0:T(8,128)}, u32[]{:S(2)}) copy-start(f32[288,1152]{1,0:T(8,128)} %get-tuple-element.11) | copy-start | bytes 3981316
  168.8 1.7 copy-start.2

commit v3 on v2

--- a/solution.py
+++ b/solution.py
@@ -362,16 +362,14 @@
     own_terms(2, is_far)
     spare = list(range(1, n_col))
     partner_terms(0)
+    partner_terms(1)
     input_part(spare.pop(0))
     own_terms(0)
-    if spare:
+    own_terms(1)
+    while spare:
         input_part(spare.pop(0))
-    partner_terms(1)
     for p in later:
         second(p)
-    while spare:
-        input_part(spare.pop(0))
-    own_terms(1)
     input_part(0)
     for p in range(len(pieces)):
         if p not in later:

time: 171 us -> 170 us (level)
  Pallas kernels: 166 us -> 164 us
where the time goes in v3:
time: 170 us
  Pallas kernels  164 us (96%)
  other arithmetic  4.29 us (3%)
    pallas_call x1, Pallas kernels, body(): pl.pallas_call(functools.partial(kernel, sizes), out_shape=[jax.ShapeDtyp...  164 us

profile of v3, /device:TPU:0, one launch (start us, length us, event | category | flops | bytes accessed | tf_op | source)
XLA Modules:
  0.0 170.3 jit_solution(2866985986361325766)
XLA Ops:
  0.6 164.5 %shard_map.84 = (bf16[576,512]{1,0:T(8,128)(2,1)}, f32[288,1152]{1,0:T(8,128)}, f32[288,1152]{1,0:T(8,128)}, f32[288,1152]{1,0:T(8,128)}) custom-call(bf16[576,512]{1,0:T(8,128)(2,1)} %bitcast.8, bf16[576,512]{1,0:T(8,128)(2,1)} %bitcast.9, bf16[288,1152]{1,0:T(8,128)(2,1)} %wg_ref.1, bf16[288,1152]{1,0:T(8,128)(2,1)} %wu_ref.1, bf16[288,1152]{1,0:T(8,128)(2,1)} %bitcast.6), custom_call_target="tpu_custom_call" | custom-call | tf_op jit(solution)/shard_map/pallas_call | solution.py:413
  165.1 0.0 copy-start
  165.1 0.0 copy-start.1
  165.1 2.6 %broadcast_multiply_fusion.1 = f32[288,1152]{1,0:T(8,128)} fusion(f32[288,1152]{1,0:T(8,128)} %get-tuple-element.9), kind=kLoop, calls=%fused_computation.2 | loop fusion | flops 331776 | bytes 2654208 | tf_op jit(solution)/shard_map/mul | solution.py:437
  167.8 0.0 copy-done
  167.8 0.0 copy-done.1
  167.8 0.0 copy-start.2
  167.8 1.7 multiply_bitcast_fusion
  169.4 0.0 copy-done.2
  169.4 0.8 copy.10
Async XLA Ops:
  165.1 2.6 %copy-start = (f32[288,1152]{1,0:T(8,128)S(1)}, f32[288,1152]{1,0:T(8,128)}, u32[]{:S(2)}) copy-start(f32[288,1152]{1,0:T(8,128)} %get-tuple-element.10) | copy-start | bytes 3981316
  165.1 2.6 %copy-start.1 = (f32[288,1152]{1,0:T(8,128)S(1)}, f32[288,1152]{1,0:T(8,128)}, u32[]{:S(2)}) copy-start(f32[288,1152]{1,0:T(8,128)} %get-tuple-element.11) | copy-start | bytes 3981316
  167.8 1.7 copy-start.2
